TPU v7x, 32 devices: a whole 2x2x4 slice. The times are simulated.
32 devices in a mesh: gx: 2 (over x), gy: 4 (over z), gz: 4 (over y, core).
Axes of the slice: x: 2, y: 2, z: 4, core: 2. Of those that a mesh axis runs over, the one named last changes fastest.
Arguments:
- acts: bfloat16 [40960, 768], P(('gx', 'gy', 'gz')), may hold values from -6 to 6
- grads_out: bfloat16 [40960, 768], P(('gx', 'gy', 'gz')), may hold values from -0.03125 to 0.03125
- master: float32 [4608, 128], P(('gx', 'gy', 'gz')), may hold values from -0.3 to 0.3
- moment: float32 [4608, 128], P(('gx', 'gy', 'gz')), may hold values from -6 to 6
- second: float32 [4608, 128], P(('gx', 'gy', 'gz')), may hold values from 0.1 to 2
Outputs:
- master_new: float32 [4608, 128], P(('gx', 'gy', 'gz'))
- moment_new: float32 [4608, 128], P(('gx', 'gy', 'gz'))
- second_new: float32 [4608, 128], P(('gx', 'gy', 'gz'))
- weights: bfloat16 [768, 768], replicated
All inputs are finite; a program needn't handle non-finite values.
Results may differ from a plain program's by a relative error of at most 0.003.
Values may be sent and summed in bfloat16 or wider, within the bound.
No kernel may reach another device: no remote copies, remote signals or barrier semaphores. Data moves between devices by JAX's collectives and lax.ppermute only.
A program may use at most 64 MiB of HBM per device.

v0:
```python
import jax
import jax.numpy as jnp
from jax import lax
from jax.sharding import PartitionSpec as P

STEP = 1000


def shards(acts, grads_out, master, moment, second):
    width_in = acts.shape[1]
    width_out = grads_out.shape[1]
    lane = master.shape[1]
    total_rows = width_in * width_out // lane
    local_grad = lax.dot_general(
        acts, grads_out, (((0,), (0,)), ((), ())), preferred_element_type=jnp.float32
    )
    local_flat = local_grad.reshape(total_rows, lane)
    partial_value = lax.psum_scatter(
        local_flat.astype(jnp.bfloat16), "gx", scatter_dimension=0, tiled=True
    ).astype(jnp.float32)
    partial_value = lax.psum_scatter(
        partial_value.astype(jnp.bfloat16), "gy", scatter_dimension=0, tiled=True
    ).astype(jnp.float32)
    gradient = lax.psum_scatter(
        partial_value.astype(jnp.bfloat16), "gz", scatter_dimension=0, tiled=True
    ).astype(jnp.float32)
    moment_new = 0.9 * moment + 0.1 * gradient
    second_new = 0.95 * second + 0.05 * gradient * gradient
    first_fix = 1.0 - 0.9**STEP
    second_fix = 1.0 - 0.95**STEP
    ratio = moment_new / first_fix / (jnp.sqrt(second_new / second_fix) + 1e-08)
    master_new = master - 0.01 * (ratio + 0.01 * master)
    rounded = master_new.astype(jnp.bfloat16)
    gathered = lax.all_gather(rounded, "gz", axis=0, tiled=True)
    gathered = lax.all_gather(gathered, "gy", axis=0, tiled=True)
    gathered = lax.all_gather(gathered, "gx", axis=0, tiled=True)
    weights = gathered.reshape(width_in, width_out)
    return (master_new, moment_new, second_new, weights)


def solution(mesh):
    return jax.shard_map(
        shards,
        mesh=mesh,
        in_specs=(
            P(("gx", "gy", "gz"), None),
            P(("gx", "gy", "gz"), None),
            P(("gx", "gy", "gz"), None),
            P(("gx", "gy", "gz"), None),
            P(("gx", "gy", "gz"), None),
        ),
        out_specs=(
            P(("gx", "gy", "gz"), None),
            P(("gx", "gy", "gz"), None),
            P(("gx", "gy", "gz"), None),
            P(),
        ),
        check_vma=False,
    )
```

profile of v0, /device:TPU:0, one launch (start us, length us, event | category | flops | bytes accessed | tf_op | source)
XLA Modules:
  0.0 141.0 jit_solution(13236243267090482629)
XLA Ops:
  7.2 0.0 copy-start
  7.2 0.0 reduce-scatter.4.cloned.1.call-start
  7.2 1.5 %copy-done = bf16[1280,768]{1,0:T(8,128)(2,1)S(1)} copy-done((bf16[1280,768]{1,0:T(8,128)(2,1)S(1)}, bf16[1280,768]{1,0:T(8,128)(2,1)}, u32[]{:S(2)}) %copy-start) | copy-done | bytes 1966104
  8.7 3.3 %convolution_convert_fusion = bf16[768,768]{1,0:T(8,128)(2,1)S(1)} fusion(bf16[1280,768]{1,0:T(8,128)(2,1)S(1)} %copy-done, bf16[1280,768]{1,0:T(8,128)(2,1)} %param.6), kind=kOutput, calls=%fused_computation | convolution fusion | flops 1510539264 | bytes 5111808 | tf_op jit(solution)/shard_map/dot_general | solution.py:14
  12.0 0.0 copy-start.1
  12.0 0.0 copy-start.2
  12.0 0.0 copy-start.3
  12.1 1.9 %convert_element_type.17 = bf16[4608,128]{1,0:T(8,128)(2,1)} reshape(bf16[768,768]{1,0:T(8,128)(2,1)S(1)} %convolution_convert_fusion) | data formatting | bytes 2359296 | tf_op jit(solution)/shard_map/convert_element_type | solution.py:19
  13.9 0.0 reduce-scatter.4.cloned.1.call-update
  13.9 0.0 reduce-scatter.6.cloned.1.call-start
  14.0 24.7 %reduce-scatter.4.cloned.1.call-done = bf16[2304,128]{1,0:T(8,128)(2,1)} async-done(((bf16[4608,128]{1,0:T(8,128)(2,1)}), bf16[2304,128]{1,0:T(8,128)(2,1)}) %reduce-scatter.4.cloned.1.call-update) | async-done | bytes 589840 | tf_op jit(solution)/shard_map/reduce_scatter | solution.py:18
  38.7 0.0 reduce-scatter.6.cloned.1.call-update
  38.7 0.0 reduce-scatter.8.cloned.1.call-start
  38.7 24.4 %reduce-scatter.6.cloned.1.call-done = bf16[576,128]{1,0:T(8,128)(2,1)} async-done(((bf16[2304,128]{1,0:T(8,128)(2,1)}), bf16[576,128]{1,0:T(8,128)(2,1)}) %reduce-scatter.6.cloned.1.call-update) | async-done | bytes 147472 | tf_op jit(solution)/shard_map/reduce_scatter | solution.py:21
  63.1 0.0 reduce-scatter.8.cloned.1.call-update
  63.1 0.0 all-gather.2.cloned.1.call-start
  63.2 20.5 %reduce-scatter.8.cloned.1.call-done = bf16[144,128]{1,0:T(8,128)(2,1)} async-done(((bf16[576,128]{1,0:T(8,128)(2,1)}), bf16[144,128]{1,0:T(8,128)(2,1)}) %reduce-scatter.8.cloned.1.call-update) | async-done | bytes 36880 | tf_op jit(solution)/shard_map/reduce_scatter | solution.py:24
  83.7 0.0 copy-done.1
  83.7 0.0 copy-done.2
  83.7 0.0 copy-done.3
  83.7 1.5 %fusion.2 = (bf16[144,128]{1,0:T(8,128)(2,1)S(1)}, f32[144,128]{1,0:T(8,128)}, f32[144,128]{1,0:T(8,128)}, f32[144,128]{1,0:T(8,128)}) fusion(f32[144,128]{1,0:T(8,128)S(1)} %copy-done.1, bf16[144,128]{1,0:T(8,128)(2,1)} %reduce-scatter.8.cloned.1.call-done, f32[144,128]{1,0:T(8,128)S(1)} %copy-done.2, f32[144,128]{1,0:T(8,128)S(1)} %copy-done.3), kind=kLoop, calls=%fused_computation.6 | loop fusion | flops 276480 | bytes 516096 | tf_op jit(solution)/shard_map/convert_element_type | solution.py:33
  85.2 5.4 %all_gather.9 = bf16[576,128]{1,0:T(8,128)(2,1)S(1)} all-gather(bf16[144,128]{1,0:T(8,128)(2,1)S(1)} %get-tuple-element.4), channel_id=1, replica_groups=mesh['gx'=2,'gy'=4,'gz'=4] {'gz'}, dimensions={0}, use_global_device_ids=true | all-gather | bytes 184320 | tf_op jit(solution)/shard_map/all_gather | solution.py:34
  90.6 17.2 %all_gather.10 = bf16[2304,128]{1,0:T(8,128)(2,1)} all-gather(bf16[576,128]{1,0:T(8,128)(2,1)S(1)} %all_gather.9), channel_id=1, replica_groups=mesh['gx'=2,'gy'=4,'gz'=4] {'gy'}, dimensions={0}, use_global_device_ids=true | all-gather | bytes 737280 | tf_op jit(solution)/shard_map/all_gather | solution.py:35
  107.8 0.0 all-gather.2.cloned.1.call-update
  107.8 23.3 %all-gather.2.cloned.1.call-done = bf16[4608,128]{1,0:T(8,128)(2,1)} async-done(((bf16[2304,128]{1,0:T(8,128)(2,1)}), bf16[4608,128]{1,0:T(8,128)(2,1)}) %all-gather.2.cloned.1.call-update) | async-done | bytes 1179664 | tf_op jit(solution)/shard_map/all_gather | solution.py:36
  131.1 3.3 %reshape.13 = bf16[768,768]{1,0:T(8,128)(2,1)} reshape(bf16[4608,128]{1,0:T(8,128)(2,1)} %all-gather.2.cloned.1.call-done) | data formatting | bytes 2359296 | tf_op jit(solution)/shard_map/reshape | solution.py:37
Async XLA Ops:
  7.2 1.6 %copy-start = (bf16[1280,768]{1,0:T(8,128)(2,1)S(1)}, bf16[1280,768]{1,0:T(8,128)(2,1)}, u32[]{:S(2)}) copy-start(bf16[1280,768]{1,0:T(8,128)(2,1)} %param.5) | copy-start | bytes 5898244
  7.2 31.5 %reduce-scatter.4.cloned.1.call-start = ((), (), s32[]{:S(2)}) async-start(), calls=%async_computation.3 | async-start | bytes 1769472 | tf_op jit(solution)/shard_map/reduce_scatter | solution.py:18
  12.0 71.7 %copy-start.1 = (f32[144,128]{1,0:T(8,128)S(1)}, f32[144,128]{1,0:T(8,128)}, u32[]{:S(2)}) copy-start(f32[144,128]{1,0:T(8,128)} %param.7) | copy-start | bytes 221188
  12.0 71.7 %copy-start.2 = (f32[144,128]{1,0:T(8,128)S(1)}, f32[144,128]{1,0:T(8,128)}, u32[]{:S(2)}) copy-start(f32[144,128]{1,0:T(8,128)} %param.9) | copy-start | bytes 221188
  12.0 71.7 %copy-start.3 = (f32[144,128]{1,0:T(8,128)S(1)}, f32[144,128]{1,0:T(8,128)}, u32[]{:S(2)}) copy-start(f32[144,128]{1,0:T(8,128)} %param.8) | copy-start | bytes 221188
  13.9 49.2 %reduce-scatter.6.cloned.1.call-start = ((), (), s32[]{:S(2)}) async-start(), calls=%async_computation.4 | async-start | bytes 737280 | tf_op jit(solution)/shard_map/reduce_scatter | solution.py:21
  38.7 45.0 %reduce-scatter.8.cloned.1.call-start = ((), (), s32[]{:S(2)}) async-start(), calls=%async_computation.5 | async-start | bytes 184320 | tf_op jit(solution)/shard_map/reduce_scatter | solution.py:24
  63.1 68.0 %all-gather.2.cloned.1.call-start = ((), (), s32[]{:S(2)}) async-start(), calls=%async_computation.6 | async-start | bytes 1769472 | tf_op jit(solution)/shard_map/all_gather | solution.py:36
Sparse Core Ops, SparseCore 0:
  14.1 24.5 reduce-scatter.3
  40.9 22.1 reduce-scatter.5
  65.5 18.1 reduce-scatter.7
  108.0 23.0 all-gather.1
where the time goes:
time: 141 us
  waiting for transfers between devices  92.9 us (66%)
  blocking collectives  22.6 us (16%)
  between operations  13.8 us (10%)
  local copies, waits for them, and re-layouts  6.73 us (5%)
  matrix products  3.29 us (2%)
  other arithmetic  1.48 us (1%)
    reduce_scatter x1, waiting for transfers between devices, shards(): lax.psum_scatter(local_flat.astype(jnp.bfloat16), 'gx', scatter_dimension...  24.7 us
    reduce_scatter x1, waiting for transfers between devices, shards(): lax.psum_scatter(partial_value.astype(jnp.bfloat16), 'gy', scatter_dimens...  24.4 us
    all_gather x1, waiting for transfers between devices, shards(): gathered = lax.all_gather(gathered, 'gx', axis=0, tiled=True)  23.3 us
    reduce_scatter x1, waiting for transfers between devices, shards(): lax.psum_scatter(partial_value.astype(jnp.bfloat16), 'gz', scatter_dimens...  20.5 us
    all_gather x1, blocking collectives, shards(): gathered = lax.all_gather(gathered, 'gy', axis=0, tiled=True)  17.2 us
    all_gather x1, blocking collectives, shards(): gathered = lax.all_gather(rounded, 'gz', axis=0, tiled=True)  5.45 us
    reshape x1, local copies, waits for them, and re-layouts, shards(): weights = gathered.reshape(width_in, width_out)  3.35 us
    dot_general x1, matrix products, shards(): lax.dot_general(acts, grads_out, (((0,), (0,)), ((), ())), preferred_elem...  3.29 us
  transfers between devices with their start and end apart: 4, of which 4 were waited for; matrix products, arithmetic and copies ran while one was open for 0% of the time, Pallas kernels for 0%

commit v1 on v0

--- a/solution.py
+++ b/solution.py
@@ -4,6 +4,16 @@
 from jax.sharding import PartitionSpec as P
 
 STEP = 1000
+
+
+def pass_along(x, name, along):
+    size = lax.axis_size(name)
+    block, pieces = (x, [x])
+    for _ in range(size - 1):
+        block = lax.ppermute(block, name, [(i, (i + 1) % size) for i in range(size)])
+        pieces.insert(0, block)
+    flat = jnp.concatenate(pieces, axis=along)
+    return jnp.roll(flat, (lax.axis_index(name) + 1) * x.shape[along], axis=along)
 
 
 def shards(acts, grads_out, master, moment, second):
@@ -32,7 +42,7 @@
     master_new = master - 0.01 * (ratio + 0.01 * master)
     rounded = master_new.astype(jnp.bfloat16)
     gathered = lax.all_gather(rounded, "gz", axis=0, tiled=True)
-    gathered = lax.all_gather(gathered, "gy", axis=0, tiled=True)
+    gathered = pass_along(gathered, "gy", 0)
     gathered = lax.all_gather(gathered, "gx", axis=0, tiled=True)
     weights = gathered.reshape(width_in, width_out)
     return (master_new, moment_new, second_new, weights)

time: 141 us -> 144 us (1.021)
  blocking collectives: 22.6 us -> 5.45 us
  waiting for transfers between devices: 92.9 us -> 110 us
  starting transfers between devices: 0.16 us -> 1.64 us
    ppermute x0 -> x3, waiting for transfers between devices: none -> 20.4 us  [pass_along(): lax.ppermute(block, name, [(i, (i + 1) % size) for i in range(size)])]
    all_gather x1 -> x0, blocking collectives: 17.2 us -> none  [shards(): gathered = lax.all_gather(gathered, 'gy', axis=0, tiled=True)]
    all_gather x1, waiting for transfers between devices: 23.3 us -> 20.2 us  [shards(): gathered = lax.all_gather(gathered, 'gx', axis=0, tiled=True)]
    ppermute x0 -> x3, starting transfers between devices: none -> 1.49 us  [pass_along(): lax.ppermute(block, name, [(i, (i + 1) % size) for i in range(size)])]
  transfers between devices with their start and end apart: 4 -> 7, of which waited for: 4 -> 7; matrix products, arithmetic and copies ran while one was open for 0% -> 0% of each run, Pallas kernels for 0% -> 0%
where the time goes in v1:
time: 144 us
  waiting for transfers between devices  110 us (76%)
  between operations  13.8 us (10%)
  local copies, waits for them, and re-layouts  7.86 us (5%)
  blocking collectives  5.45 us (4%)
  matrix products  3.29 us (2%)
  starting transfers between devices  1.64 us (1%)
  other arithmetic  1.48 us (1%)
    reduce_scatter x1, waiting for transfers between devices, shards(): lax.psum_scatter(local_flat.astype(jnp.bfloat16), 'gx', scatter_dimension...  24.7 us
    reduce_scatter x1, waiting for transfers between devices, shards(): lax.psum_scatter(partial_value.astype(jnp.bfloat16), 'gy', scatter_dimens...  24.4 us
    reduce_scatter x1, waiting for transfers between devices, shards(): lax.psum_scatter(partial_value.astype(jnp.bfloat16), 'gz', scatter_dimens...  20.5 us
    ppermute x3, waiting for transfers between devices, pass_along(): lax.ppermute(block, name, [(i, (i + 1) % size) for i in range(size)])  20.4 us
    all_gather x1, waiting for transfers between devices, shards(): gathered = lax.all_gather(gathered, 'gx', axis=0, tiled=True)  20.2 us
    all_gather x1, blocking collectives, shards(): gathered = lax.all_gather(rounded, 'gz', axis=0, tiled=True)  5.45 us
    reshape x1, local copies, waits for them, and re-layouts, shards(): weights = gathered.reshape(width_in, width_out)  3.35 us
    dot_general x1, matrix products, shards(): lax.dot_general(acts, grads_out, (((0,), (0,)), ((), ())), preferred_elem...  3.29 us
  transfers between devices with their start and end apart: 7, of which 7 were waited for; matrix products, arithmetic and copies ran while one was open for 0% of the time, Pallas kernels for 0%

profile of v1, /device:TPU:0, one launch (start us, length us, event | category | flops | bytes accessed | tf_op | source)
XLA Modules:
  0.0 143.7 jit_solution(3440438258364149620)
XLA Ops:
  7.2 0.0 copy-start
  7.2 0.0 reduce-scatter.4.cloned.1.call-start
  7.2 1.5 %copy-done = bf16[1280,768]{1,0:T(8,128)(2,1)S(1)} copy-done((bf16[1280,768]{1,0:T(8,128)(2,1)S(1)}, bf16[1280,768]{1,0:T(8,128)(2,1)}, u32[]{:S(2)}) %copy-start) | copy-done | bytes 1966104
  8.7 3.3 %convolution_convert_fusion = bf16[768,768]{1,0:T(8,128)(2,1)S(1)} fusion(bf16[1280,768]{1,0:T(8,128)(2,1)S(1)} %copy-done, bf16[1280,768]{1,0:T(8,128)(2,1)} %param.6), kind=kOutput, calls=%fused_computation | convolution fusion | flops 1510539264 | bytes 5111808 | tf_op jit(solution)/shard_map/dot_general | solution.py:24
  12.0 1.9 %convert_element_type.17 = bf16[4608,128]{1,0:T(8,128)(2,1)} reshape(bf16[768,768]{1,0:T(8,128)(2,1)S(1)} %convolution_convert_fusion) | data formatting | bytes 2359296 | tf_op jit(solution)/shard_map/convert_element_type | solution.py:29
  13.9 0.0 copy-start.1
  13.9 0.0 copy-start.2
  13.9 0.0 copy-start.3
  13.9 0.0 reduce-scatter.4.cloned.1.call-update
  13.9 0.0 reduce-scatter.6.cloned.1.call-start
  14.0 24.7 %reduce-scatter.4.cloned.1.call-done = bf16[2304,128]{1,0:T(8,128)(2,1)} async-done(((bf16[4608,128]{1,0:T(8,128)(2,1)}), bf16[2304,128]{1,0:T(8,128)(2,1)}) %reduce-scatter.4.cloned.1.call-update) | async-done | bytes 589840 | tf_op jit(solution)/shard_map/reduce_scatter | solution.py:28
  38.6 0.0 reduce-scatter.6.cloned.1.call-update
  38.6 0.0 reduce-scatter.8.cloned.1.call-start
  38.7 24.4 %reduce-scatter.6.cloned.1.call-done = bf16[576,128]{1,0:T(8,128)(2,1)} async-done(((bf16[2304,128]{1,0:T(8,128)(2,1)}), bf16[576,128]{1,0:T(8,128)(2,1)}) %reduce-scatter.6.cloned.1.call-update) | async-done | bytes 147472 | tf_op jit(solution)/shard_map/reduce_scatter | solution.py:31
  63.1 0.0 reduce-scatter.8.cloned.1.call-update
  63.1 0.0 all-gather.2.cloned.1.call-start
  63.1 20.5 %reduce-scatter.8.cloned.1.call-done = bf16[144,128]{1,0:T(8,128)(2,1)} async-done(((bf16[576,128]{1,0:T(8,128)(2,1)}), bf16[144,128]{1,0:T(8,128)(2,1)}) %reduce-scatter.8.cloned.1.call-update) | async-done | bytes 36880 | tf_op jit(solution)/shard_map/reduce_scatter | solution.py:34
  83.7 0.0 copy-done.1
  83.7 0.0 copy-done.2
  83.7 0.0 copy-done.3
  83.7 1.5 %fusion.2 = (bf16[144,128]{1,0:T(8,128)(2,1)S(1)}, f32[144,128]{1,0:T(8,128)}, f32[144,128]{1,0:T(8,128)}, f32[144,128]{1,0:T(8,128)}) fusion(f32[144,128]{1,0:T(8,128)S(1)} %copy-done.1, bf16[144,128]{1,0:T(8,128)(2,1)} %reduce-scatter.8.cloned.1.call-done, f32[144,128]{1,0:T(8,128)S(1)} %copy-done.2, f32[144,128]{1,0:T(8,128)S(1)} %copy-done.3), kind=kLoop, calls=%fused_computation.15 | loop fusion | flops 276480 | bytes 516096 | tf_op jit(solution)/shard_map/convert_element_type | solution.py:43
  85.1 5.4 %all_gather.6 = bf16[576,128]{1,0:T(8,128)(2,1)S(1)} all-gather(bf16[144,128]{1,0:T(8,128)(2,1)S(1)} %get-tuple-element.4), channel_id=1, replica_groups=mesh['gx'=2,'gy'=4,'gz'=4] {'gz'}, dimensions={0}, use_global_device_ids=true | all-gather | bytes 184320 | tf_op jit(solution)/shard_map/all_gather | solution.py:44
  90.6 1.5 %collective-permute-start = (bf16[576,128]{1,0:T(8,128)(2,1)S(1)}, bf16[576,128]{1,0:T(8,128)(2,1)S(1)}, u32[]{:S(2)}, u32[]{:S(2)}) collective-permute-start(bf16[576,128]{1,0:T(8,128)(2,1)S(1)} %all_gather.6), channel_id=1, source_target_pairs={{0,4},{4,8},{8,12},{12,0},{1,5},{5,9},{9,13},{13,1},{2,6},{6,10},{... | collective-permute-start | bytes 442376 | tf_op jit(solution)/shard_map/ppermute | solution.py:13
  92.1 6.4 %collective-permute-done = bf16[576,128]{1,0:T(8,128)(2,1)S(1)} collective-permute-done((bf16[576,128]{1,0:T(8,128)(2,1)S(1)}, bf16[576,128]{1,0:T(8,128)(2,1)S(1)}, u32[]{:S(2)}, u32[]{:S(2)}) %collective-permute-start) | collective-permute-done | bytes 147488 | tf_op jit(solution)/shard_map/ppermute | solution.py:13
  98.5 0.0 collective-permute-start.1
  98.5 7.0 %collective-permute-done.1 = bf16[576,128]{1,0:T(8,128)(2,1)S(1)} collective-permute-done((bf16[576,128]{1,0:T(8,128)(2,1)S(1)}, bf16[576,128]{1,0:T(8,128)(2,1)S(1)}, u32[]{:S(2)}, u32[]{:S(2)}) %collective-permute-start.1) | collective-permute-done | bytes 147488 | tf_op jit(solution)/shard_map/ppermute | solution.py:13
  105.5 0.0 collective-permute-start.2
  105.5 6.9 %collective-permute-done.2 = bf16[576,128]{1,0:T(8,128)(2,1)S(1)} collective-permute-done((bf16[576,128]{1,0:T(8,128)(2,1)S(1)}, bf16[576,128]{1,0:T(8,128)(2,1)S(1)}, u32[]{:S(2)}, u32[]{:S(2)}) %collective-permute-start.2) | collective-permute-done | bytes 147488 | tf_op jit(solution)/shard_map/ppermute | solution.py:13
  112.7 1.0 constant_dynamic-slice_fusion
  113.7 0.0 all-gather.2.cloned.1.call-update
  113.7 20.2 %all-gather.2.cloned.1.call-done = bf16[4608,128]{1,0:T(8,128)(2,1)} async-done(((bf16[2304,128]{1,0:T(8,128)(2,1)}), bf16[4608,128]{1,0:T(8,128)(2,1)}) %all-gather.2.cloned.1.call-update) | async-done | bytes 1179664 | tf_op jit(solution)/shard_map/all_gather | solution.py:46
  133.8 3.3 %reshape.13 = bf16[768,768]{1,0:T(8,128)(2,1)} reshape(bf16[4608,128]{1,0:T(8,128)(2,1)} %all-gather.2.cloned.1.call-done) | data formatting | bytes 2359296 | tf_op jit(solution)/shard_map/reshape | solution.py:47
  (8 shorter events, 0.2 us)
Async XLA Ops:
  7.2 1.6 %copy-start = (bf16[1280,768]{1,0:T(8,128)(2,1)S(1)}, bf16[1280,768]{1,0:T(8,128)(2,1)}, u32[]{:S(2)}) copy-start(bf16[1280,768]{1,0:T(8,128)(2,1)} %param.5) | copy-start | bytes 5898244
  7.2 31.4 %reduce-scatter.4.cloned.1.call-start = ((), (), s32[]{:S(2)}) async-start(), calls=%async_computation.3 | async-start | bytes 1769472 | tf_op jit(solution)/shard_map/reduce_scatter | solution.py:28
  13.9 69.8 %copy-start.1 = (f32[144,128]{1,0:T(8,128)S(1)}, f32[144,128]{1,0:T(8,128)}, u32[]{:S(2)}) copy-start(f32[144,128]{1,0:T(8,128)} %param.7) | copy-start | bytes 221188
  13.9 69.8 %copy-start.2 = (f32[144,128]{1,0:T(8,128)S(1)}, f32[144,128]{1,0:T(8,128)}, u32[]{:S(2)}) copy-start(f32[144,128]{1,0:T(8,128)} %param.9) | copy-start | bytes 221188
  13.9 69.8 %copy-start.3 = (f32[144,128]{1,0:T(8,128)S(1)}, f32[144,128]{1,0:T(8,128)}, u32[]{:S(2)}) copy-start(f32[144,128]{1,0:T(8,128)} %param.8) | copy-start | bytes 221188
  13.9 49.2 %reduce-scatter.6.cloned.1.call-start = ((), (), s32[]{:S(2)}) async-start(), calls=%async_computation.4 | async-start | bytes 737280 | tf_op jit(solution)/shard_map/reduce_scatter | solution.py:31
  38.6 45.0 %reduce-scatter.8.cloned.1.call-start = ((), (), s32[]{:S(2)}) async-start(), calls=%async_computation.5 | async-start | bytes 184320 | tf_op jit(solution)/shard_map/reduce_scatter | solution.py:34
  63.1 70.7 %all-gather.2.cloned.1.call-start = ((), (), s32[]{:S(2)}) async-start(), calls=%async_computation.6 | async-start | bytes 1769472 | tf_op jit(solution)/shard_map/all_gather | solution.py:46
  90.6 7.9 %collective-permute-start = (bf16[576,128]{1,0:T(8,128)(2,1)S(1)}, bf16[576,128]{1,0:T(8,128)(2,1)S(1)}, u32[]{:S(2)}, u32[]{:S(2)}) collective-permute-start(bf16[576,128]{1,0:T(8,128)(2,1)S(1)} %all_gather.6), channel_id=1, source_target_pairs={{0,4},{4,8},{8,12},{12,0},{1,5},{5,9},{9,13},{13,1},{2,6},{6,10},{... | collective-permute-start | bytes 442376 | tf_op jit(solution)/shard_map/ppermute | solution.py:13
  98.5 7.0 %collective-permute-start.1 = (bf16[576,128]{1,0:T(8,128)(2,1)S(1)}, bf16[576,128]{1,0:T(8,128)(2,1)S(1)}, u32[]{:S(2)}, u32[]{:S(2)}) collective-permute-start(bf16[576,128]{1,0:T(8,128)(2,1)S(1)} %collective-permute-done), channel_id=1, source_target_pairs={{0,4},{4,8},{8,12},{12,0},{1,5},{5,9},{9,13},{13,1},{2,6},{6,10},{... | collective-permute-start | bytes 442376 | tf_op jit(solution)/shard_map/ppermute | solution.py:13
  105.5 6.9 %collective-permute-start.2 = (bf16[576,128]{1,0:T(8,128)(2,1)S(1)}, bf16[576,128]{1,0:T(8,128)(2,1)S(1)}, u32[]{:S(2)}, u32[]{:S(2)}) collective-permute-start(bf16[576,128]{1,0:T(8,128)(2,1)S(1)} %collective-permute-done.1), channel_id=1, source_target_pairs={{0,4},{4,8},{8,12},{12,0},{1,5},{5,9},{9,13},{13,1},{2,6},{6,10},{... | collective-permute-start | bytes 442376 | tf_op jit(solution)/shard_map/ppermute | solution.py:13
Sparse Core Ops, SparseCore 0:
  14.0 24.5 reduce-scatter.3
  40.9 22.1 reduce-scatter.5
  65.5 18.1 reduce-scatter.7
  113.8 19.9 all-gather.1
